TPU v7x, 32 devices: a whole 2x2x4 slice. The times are simulated.
32 devices in a mesh: groups: 2 (over y), ep: 4 (over z), tp: 4 (over x, core).
Axes of the slice: x: 2, y: 2, z: 4, core: 2. Of those that a mesh axis runs over, the one named last changes fastest.
Arguments:
- context: bfloat16 [512, 4096], P(('groups', 'ep'), 'tp'), parts along dimension 0, may hold values from -6 to 6
- stream: bfloat16 [512, 4096], P(('groups', 'ep'), 'tp'), parts along dimension 0, may hold values from -14 to 14
- out_proj: bfloat16 [4096, 4096], P('tp', 'ep'), may hold values from -0.09375 to 0.09375
- norm_gain: bfloat16 [4096], P('tp'), may hold values from 0.099609375 to 1.8984375
- router: bfloat16 [4096, 4], P('tp'), may hold values from -0.0625 to 0.0625
- expert_ids: int32 [512, 2], P(('groups', 'ep')), parts along dimension 0, may hold values from 0 to 3, all different within a row; in each aligned block of 64 rows (0 to 63, 64 to 127, ...) at most 36 rows name the same one
- w_gate: bfloat16 [4096, 28672], P('tp', 'ep'), may hold values from -0.09375 to 0.09375
- w_up: bfloat16 [4096, 28672], P('tp', 'ep'), may hold values from -0.09375 to 0.09375
- w_down: bfloat16 [28672, 4096], P('ep', 'tp'), may hold values from -0.125 to 0.125
Outputs:
- layer_out: bfloat16 [512, 4096], P(('groups', 'ep'), 'tp'), parts along dimension 0
There are 2 independent parts, one for each index of `groups`. A program takes and returns all parts, laid end to end along the dimension named above; an argument that names none is the same for every part. Nothing has to cross between parts.
Inputs may be any that keep to these rules, and one draw needn't show every extreme that they name: `expert_ids`: each row names 2 different experts. In each aligned block of 64 rows (the rows of one index of ep) no expert is named by more than 36 rows, and in some blocks one expert is named by exactly 36 rows.
All inputs are finite; a program needn't handle non-finite values.
Results may differ from a plain program's by a relative error of at most 0.02.
Values may be sent and summed in bfloat16 or wider, within the bound.
A program may use at most 128 MiB of HBM per device.

v0:
```python
import jax
import jax.numpy as jnp
from jax import lax
from jax.sharding import PartitionSpec as P

D = 4096
EXPERTS = 4
CAP = 36


def per_device(context, stream, out_proj, norm_gain, router, expert_ids, w_gate, w_up, w_down):
    tok_rows = stream.shape[0]
    width_part = stream.shape[1]
    ep_count = lax.axis_size("ep")
    fanout = ep_count // EXPERTS
    columns = jnp.dot(
        lax.all_gather(context, "ep", axis=0, tiled=True),
        out_proj,
        preferred_element_type=jnp.float32,
    )
    head_part = lax.all_to_all(
        columns.astype(jnp.bfloat16), "ep", split_axis=0, concat_axis=1, tiled=True
    )
    attention = lax.psum_scatter(head_part, "tp", scatter_dimension=1, tiled=True).astype(
        jnp.float32
    )
    hstate = (stream.astype(jnp.float32) + attention).astype(jnp.bfloat16)
    hfloat = hstate.astype(jnp.float32)
    gain_vec = norm_gain.astype(jnp.float32)
    router_wide = router.astype(jnp.float32)
    squares = jnp.sum(hfloat * hfloat, axis=1)
    total_sq = lax.psum(squares, "tp")
    inverse = lax.rsqrt(total_sq / D + 1e-05)[:, None]
    normed = hfloat * inverse * gain_vec[None, :]
    logits = lax.psum(jnp.dot(normed, router_wide, precision=lax.Precision.HIGHEST), "tp")
    inputs = normed.astype(jnp.bfloat16)
    experts_range = jnp.arange(EXPERTS, dtype=jnp.int32)
    flat_ids = expert_ids.reshape(tok_rows * 2)
    onehot = (flat_ids[:, None] == experts_range[None, :]).astype(jnp.int32)
    before = jnp.cumsum(onehot, axis=0) - onehot
    slot_index = jnp.sum(before * onehot, axis=1)
    target = flat_ids * CAP + slot_index
    picked = onehot.reshape(tok_rows, 2, EXPERTS).astype(jnp.float32)
    chosen = jnp.sum(picked * logits[:, None, :], axis=2)
    leading = jax.nn.sigmoid(chosen[:, 0] - chosen[:, 1])
    weights = jnp.stack([leading, 1.0 - leading], axis=1)
    columns_all = jnp.arange(EXPERTS * CAP, dtype=jnp.int32)
    placement = (
        (target[:, None] == columns_all[None, :])
        .astype(jnp.float32)
        .reshape(tok_rows, 2, EXPERTS * CAP)
    )
    dispatch = jnp.sum(placement, axis=1)
    combine = jnp.sum(placement * weights[:, :, None], axis=1)
    sectioned = lax.dot_general(
        dispatch.astype(jnp.bfloat16),
        inputs,
        (((0,), (0,)), ((), ())),
        preferred_element_type=jnp.float32,
    ).astype(jnp.bfloat16)
    send_rows = jnp.broadcast_to(
        sectioned.reshape(EXPERTS, 1, CAP, width_part), (EXPERTS, fanout, CAP, width_part)
    ).reshape(ep_count, CAP, width_part)
    received = lax.all_to_all(send_rows, "ep", split_axis=0, concat_axis=0, tiled=True)
    slot_count = received.shape[1]
    flattened = received.reshape(ep_count * slot_count, width_part)
    gate_part = jnp.dot(flattened, w_gate, preferred_element_type=jnp.float32)
    up_part = jnp.dot(flattened, w_up, preferred_element_type=jnp.float32)
    gate_sum = lax.psum(gate_part.astype(jnp.bfloat16), "tp").astype(jnp.float32)
    up_sum = lax.psum(up_part.astype(jnp.bfloat16), "tp").astype(jnp.float32)
    hidden = (jax.nn.silu(gate_sum) * up_sum).astype(jnp.bfloat16)
    partial_value = jnp.dot(hidden, w_down, preferred_element_type=jnp.float32).astype(jnp.bfloat16)
    returned_rows = lax.all_to_all(
        partial_value.reshape(ep_count, slot_count, width_part),
        "ep",
        split_axis=0,
        concat_axis=0,
        tiled=True,
    )
    summed = jnp.sum(
        returned_rows.astype(jnp.float32).reshape(EXPERTS, fanout, CAP, width_part), axis=1
    ).reshape(EXPERTS * CAP, width_part)
    expert_mix = jnp.dot(combine, summed, precision=lax.Precision.HIGHEST)
    return (hfloat + expert_mix).astype(jnp.bfloat16)


def solution(mesh):
    return jax.shard_map(
        per_device,
        mesh=mesh,
        in_specs=(
            P(("groups", "ep"), "tp"),
            P(("groups", "ep"), "tp"),
            P("tp", "ep"),
            P("tp"),
            P("tp", None),
            P(("groups", "ep"), None),
            P("tp", "ep"),
            P("tp", "ep"),
            P("ep", "tp"),
        ),
        out_specs=P(("groups", "ep"), "tp"),
        check_vma=False,
    )
```

profile of v0, /device:TPU:0, one launch (start us, length us, event | category | flops | bytes accessed | tf_op | source)
XLA Modules:
  0.0 223.6 jit_solution(884350018924113710)
XLA Ops:
  6.5 0.0 copy-start
  6.5 0.0 copy-start.3
  6.5 0.0 copy-start.2
  6.5 0.0 copy-start.1
  6.5 0.0 copy-start.4
  6.5 0.0 reduce-scatter.2.cloned.1.call-start
  6.6 17.7 %all_gather.3 = bf16[256,1024]{1,0:T(8,128)(2,1)S(1)} all-gather(bf16[64,1024]{1,0:T(8,128)(2,1)} %param.9), channel_id=1, replica_groups=mesh['groups'=2,'ep'=4,'tp'=4] {'ep'}, dimensions={0}, use_global_device_ids=true | all-gather | bytes 655360 | tf_op jit(solution)/shard_map/all_gather | solution.py:17
  24.3 0.0 copy-done
  24.3 0.7 convolution_convert_fusion.2
  25.0 16.1 %all_to_all.29 = bf16[4,64,1024]{2,1,0:T(8,128)(2,1)S(1)} all-to-all(bf16[4,64,1024]{2,1,0:T(8,128)(2,1)S(1)} %bitcast.17), channel_id=1, replica_groups=mesh['groups'=2,'ep'=4,'tp'=4] {'ep'}, dimensions={0} | all-to-all | bytes 1048576 | tf_op jit(solution)/shard_map/all_to_all | solution.py:21
  41.1 0.8 copy.37
  41.9 0.0 reduce-scatter.2.cloned.1.call-update
  42.0 0.0 all-reduce.3.cloned.1.call-start
  42.0 0.0 copy-done.3
  42.0 0.0 copy-done.2
  42.0 0.1 copy.35
  42.1 0.1 eq.36
  42.3 0.1 fusion.22
  42.4 0.2 reduce_window_sum.11
  42.6 0.2 select_reduce_fusion.1
  42.7 0.1 reduce_sum.52
  42.9 0.1 copy.36
  43.0 19.9 %reduce-scatter.2.cloned.1.call-done = bf16[64,1024]{1,0:T(8,128)(2,1)} async-done(((bf16[64,4096]{1,0:T(8,128)(2,1)}), bf16[64,1024]{1,0:T(8,128)(2,1)}) %reduce-scatter.2.cloned.1.call-update) | async-done | bytes 131088 | tf_op jit(solution)/shard_map/reduce_scatter | solution.py:24
  62.9 0.0 copy-done.1
  62.9 1.1 fusion.12
  63.9 5.8 %psum.28 = f32[64]{0:T(128)S(1)} all-reduce(f32[64]{0:T(128)S(1)} %get-tuple-element.11), channel_id=1, replica_groups=mesh['groups'=2,'ep'=4,'tp'=4] {'tp'}, use_global_device_ids=true, to_apply=%region_4.0 | all-reduce | flops 64 | bytes 512 | tf_op jit(solution)/shard_map/psum | solution.py:32
  69.7 0.0 copy-done.4
  69.7 0.3 fusion.15
  70.0 5.7 %psum.29 = f32[64,4]{0,1:T(4,128)S(1)} all-reduce(f32[64,4]{0,1:T(4,128)S(1)} %fusion.15), channel_id=1, replica_groups=mesh['groups'=2,'ep'=4,'tp'=4] {'tp'}, use_global_device_ids=true, to_apply=%region_5.6 | all-reduce | flops 256 | bytes 2048 | tf_op jit(solution)/shard_map/psum | solution.py:35
  75.7 0.1 convert_reduce_fusion
  75.9 0.3 convolution_convert_fusion.3
  76.2 0.1 reshape_reshape.3
  76.2 14.9 %all_to_all.30 = bf16[4,36,1024]{2,1,0:T(8,128)(2,1)S(1)} all-to-all(bf16[4,36,1024]{2,1,0:T(8,128)(2,1)S(1)} %reshape_reshape.3), channel_id=1, replica_groups=mesh['groups'=2,'ep'=4,'tp'=4] {'ep'}, dimensions={0} | all-to-all | bytes 589824 | tf_op jit(solution)/shard_map/all_to_all | solution.py:64
  91.1 0.1 reshape.48
  91.2 8.8 %convolution_convert_fusion = bf16[144,7168]{1,0:T(8,128)(2,1)} fusion(bf16[144,1024]{1,0:T(8,128)(2,1)S(1)} %reshape.48, bf16[1024,7168]{1,0:T(8,128)(2,1)} %param.16), kind=kOutput, calls=%fused_computation | convolution fusion | flops 2114961408 | bytes 17039360 | tf_op jit(solution)/shard_map/dot_general | solution.py:68
  100.0 8.8 %convolution_convert_fusion.1 = bf16[144,7168]{1,0:T(8,128)(2,1)} fusion(bf16[144,1024]{1,0:T(8,128)(2,1)S(1)} %reshape.48, bf16[1024,7168]{1,0:T(8,128)(2,1)} %param.15), kind=kOutput, calls=%fused_computation.1 | convolution fusion | flops 2114961408 | bytes 17039360 | tf_op jit(solution)/shard_map/dot_general | solution.py:67
  108.8 0.0 all-reduce.3.cloned.1.call-update
  108.9 83.2 %all-reduce.3.cloned.1.call-done = (bf16[144,7168]{1,0:T(8,128)(2,1)}, bf16[144,7168]{1,0:T(8,128)(2,1)}) async-done(((bf16[144,7168]{1,0:T(8,128)(2,1)}, bf16[144,7168]{1,0:T(8,128)(2,1)}), (bf16[144,7168]{1,0:T(8,128)(2,1)}, bf16[144,7168]{1,0:T(8,128)(2,1)})) %all-reduce.3.cloned.1.call-update) | async-done | bytes 4128784 | tf_op jit(solution)/shard_map/psum | solution.py:70
  192.1 9.2 %fusion.8 = bf16[144,1024]{1,0:T(8,128)(2,1)S(1)} fusion(bf16[7168,1024]{1,0:T(8,128)(2,1)} %param.17, bf16[144,7168]{1,0:T(8,128)(2,1)} %get-tuple-element.7, bf16[144,7168]{1,0:T(8,128)(2,1)} %get-tuple-element.8), kind=kOutput, calls=%fused_computation.13 | convolution fusion | flops 2122334208 | bytes 19103744 | tf_op jit(solution)/shard_map/dot_general | solution.py:72
  201.3 0.1 reshape.49
  201.4 14.4 %all_to_all.31 = bf16[4,36,1024]{2,1,0:T(8,128)(2,1)S(1)} all-to-all(bf16[4,36,1024]{2,1,0:T(8,128)(2,1)S(1)} %reshape.49), channel_id=1, replica_groups=mesh['groups'=2,'ep'=4,'tp'=4] {'ep'}, dimensions={0} | all-to-all | bytes 589824 | tf_op jit(solution)/shard_map/all_to_all | solution.py:73
  215.7 0.1 reshape.50
  215.8 0.9 fusion.11
  (6 shorter events, 0.1 us)
Async XLA Ops:
  6.5 17.8 %copy-start = (bf16[1024,1024]{1,0:T(8,128)(2,1)S(1)}, bf16[1024,1024]{1,0:T(8,128)(2,1)}, u32[]{:S(2)}) copy-start(bf16[1024,1024]{1,0:T(8,128)(2,1)} %param.11) | copy-start | bytes 6291460
  6.5 35.5 %copy-start.3 = (bf16[1024]{0:T(1024)(128)(2,1)S(1)}, bf16[1024]{0:T(1024)(128)(2,1)}, u32[]{:S(2)}) copy-start(bf16[1024]{0:T(1024)(128)(2,1)} %param.12) | copy-start | bytes 6148
  6.5 35.5 %copy-start.2 = (s32[64,2]{0,1:T(2,128)S(1)}, s32[64,2]{0,1:T(2,128)}, u32[]{:S(2)}) copy-start(s32[64,2]{0,1:T(2,128)} %param.14) | copy-start | bytes 1540
  6.5 56.3 %copy-start.1 = (bf16[64,1024]{1,0:T(8,128)(2,1)S(1)}, bf16[64,1024]{1,0:T(8,128)(2,1)}, u32[]{:S(2)}) copy-start(bf16[64,1024]{1,0:T(8,128)(2,1)} %param.10) | copy-start | bytes 393220
  6.5 63.2 %copy-start.4 = (bf16[1024,4]{0,1:T(4,128)(2,1)S(1)}, bf16[1024,4]{0,1:T(4,128)(2,1)}, u32[]{:S(2)}) copy-start(bf16[1024,4]{0,1:T(4,128)(2,1)} %param.13) | copy-start | bytes 24580
  6.5 56.3 %reduce-scatter.2.cloned.1.call-start = ((), (), s32[]{:S(2)}) async-start(), calls=%async_computation.4 | async-start | bytes 655360 | tf_op jit(solution)/shard_map/reduce_scatter | solution.py:24
  42.0 150.1 %all-reduce.3.cloned.1.call-start = ((), (), s32[]{:S(2)}) async-start(), calls=%async_computation.5 | async-start | bytes 8257536 | tf_op jit(solution)/shard_map/psum | solution.py:70
Sparse Core Ops, SparseCore 0:
  42.1 20.7 reduce-scatter.1
  109.0 83.0 all-reduce.2
where the time goes:
time: 224 us
  waiting for transfers between devices  103 us (46%)
  blocking collectives  74.5 us (33%)
  matrix products  29.1 us (13%)
  between operations  13.5 us (6%)
    psum x1, waiting for transfers between devices, per_device(): up_sum = lax.psum(up_part.astype(jnp.bfloat16), 'tp').astype(jnp.float32)  83.2 us
    reduce_scatter x1, waiting for transfers between devices, per_device(): lax.psum_scatter(head_part, 'tp', scatter_dimension=1, tiled=True)  19.9 us
    all_gather x1, blocking collectives, per_device(): lax.all_gather(context, 'ep', axis=0, tiled=True)  17.7 us
    all_to_all x1, blocking collectives, per_device(): lax.all_to_all(columns.astype(jnp.bfloat16), 'ep', split_axis=0, concat_a...  16.1 us
    all_to_all x1, blocking collectives, per_device(): lax.all_to_all(send_rows, 'ep', split_axis=0, concat_axis=0, tiled=True)  14.9 us
    all_to_all x1, blocking collectives, per_device(): lax.all_to_all(partial_value.reshape(ep_count, slot_count, width_part), '...  14.4 us
    dot_general x1, matrix products, per_device(): jnp.dot(hidden, w_down, preferred_element_type=jnp.float32)  9.22 us
    dot_general x1, matrix products, per_device(): up_part = jnp.dot(flattened, w_up, preferred_element_type=jnp.float32)  8.83 us
  transfers between devices with their start and end apart: 2, of which 2 were waited for; matrix products, arithmetic and copies ran while one was open for 0% of the time, Pallas kernels for 0%

commit v1 on v0

--- a/solution.py
+++ b/solution.py
@@ -1,6 +1,10 @@
+import functools
+
 import jax
 import jax.numpy as jnp
 from jax import lax
+from jax.experimental import pallas as pl
+from jax.experimental.pallas import tpu as pltpu
 from jax.sharding import PartitionSpec as P
 
 D = 4096
@@ -8,7 +12,7 @@
 CAP = 36
 
 
-def per_device(context, stream, out_proj, norm_gain, router, expert_ids, w_gate, w_up, w_down):
+def plain_device(context, stream, out_proj, norm_gain, router, expert_ids, w_gate, w_up, w_down):
     tok_rows = stream.shape[0]
     width_part = stream.shape[1]
     ep_count = lax.axis_size("ep")
@@ -84,9 +88,480 @@
     return (hfloat + expert_mix).astype(jnp.bfloat16)
 
 
+MESH = pl.DeviceIdType.MESH
+CHUNK = 256
+WINDOW = 48
+VMEM_BYTES = 67043328
+
+
+def fused_kernel(
+    n_ep,
+    n_tp,
+    pieces,
+    ctx_ref,
+    stream_ref,
+    gain_ref,
+    router_ref,
+    ids_ref,
+    proj_hbm,
+    gate_hbm,
+    up_hbm,
+    down_hbm,
+    out_ref,
+    proj,
+    gate,
+    up,
+    down,
+    ctx_all,
+    part,
+    part_in,
+    halves,
+    landed,
+    hkeep,
+    x_all,
+    rows,
+    side,
+    side_all,
+    inv_all,
+    slot_all,
+    inv_rows,
+    pair_out,
+    pair_in,
+    own_far,
+    own_near,
+    far_out,
+    far_in,
+    hid,
+    acc,
+    outb,
+    ret,
+    w_sem,
+    ctx_send,
+    ctx_recv,
+    slot_send,
+    slot_recv,
+    part_send,
+    part_recv,
+    land_send,
+    land_recv,
+    side_send,
+    side_recv,
+    x_send,
+    x_recv,
+    inv_send,
+    inv_recv,
+    pair_send,
+    pair_recv,
+    far_send,
+    far_recv,
+    hx_send,
+    hx_recv,
+    hc_send,
+    hc_recv,
+    hf_send,
+    hf_recv,
+    ret_send,
+    ret_recv,
+):
+    me = lax.axis_index("ep")
+    lane = lax.axis_index("tp")
+    core = lax.rem(lane, 2)
+    side_x = lane // 2
+    mate = 2 * side_x + (1 - core)
+    across = 2 * (1 - side_x) + core
+    tok, width = stream_ref.shape
+    depth = n_tp * width
+    quarter = gate.shape[1] // n_tp
+    count = quarter // CHUNK
+    slots = rows.shape[0]
+    f32, bf16 = jnp.float32, jnp.bfloat16
+
+    loads = {}
+    number = 0
+    for name, src, dst in (("p", proj_hbm, proj), ("g", gate_hbm, gate), ("u", up_hbm, up), ("d", down_hbm, down)):
+        step = src.shape[0] // pieces
+        group = []
+        for p in range(pieces):
+            copy = pltpu.make_async_copy(
+                src.at[pl.ds(p * step, step)], dst.at[pl.ds(p * step, step)], w_sem.at[number]
+            )
+            copy.start()
+            group.append(copy)
+            number += 1
+        loads[name] = group
+
+    barrier = pltpu.get_barrier_semaphore()
+    for de in range(n_ep):
+        for dt in range(n_tp):
+            if de or dt:
+                pl.semaphore_signal(
+                    barrier,
+                    inc=1,
+                    device_id={"ep": lax.rem(me + de, n_ep), "tp": lax.rem(lane + dt, n_tp)},
+                    device_id_type=MESH,
+                )
+
+    ids = ids_ref[...]
+    lanes = lax.broadcasted_iota(jnp.int32, (tok, 128), 1)
+    named = jnp.where((ids[:, 0:1] == lanes) | (ids[:, 1:2] == lanes), 1.0, 0.0).astype(f32)
+    row_i = lax.broadcasted_iota(jnp.int32, (tok, tok), 0)
+    col_i = lax.broadcasted_iota(jnp.int32, (tok, tok), 1)
+    lower = jnp.where(col_i < row_i, 1.0, 0.0).astype(bf16)
+    rank = jnp.dot(lower, named.astype(bf16), preferred_element_type=f32)
+    slot_local = jnp.where(named > 0.5, rank, -4096.0)
+    slot_all[me] = slot_local
+
+    pl.semaphore_wait(barrier, n_ep * n_tp - 1)
+
+    def over_ep(src, dst, sends, recvs):
+        copies = []
+        for k in range(1, n_ep):
+            copy = pltpu.make_async_remote_copy(
+                src_ref=src,
+                dst_ref=dst,
+                send_sem=sends.at[k - 1],
+                recv_sem=recvs.at[k - 1],
+                device_id={"ep": lax.rem(me + k, n_ep)},
+                device_id_type=MESH,
+            )
+            copy.start()
+            copies.append(copy)
+        return copies
+
+    ctx_copies = over_ep(ctx_ref, ctx_all.at[me], ctx_send, ctx_recv)
+    slot_copies = over_ep(slot_all.at[me], slot_all.at[me], slot_send, slot_recv)
+
+    for copy in loads["p"]:
+        copy.wait()
+    for k in range(n_ep):
+        block = lax.rem(me + n_ep - k, n_ep)
+        if k:
+            ctx_copies[k - 1].wait_recv()
+            value = ctx_all[block]
+        else:
+            value = ctx_ref[...]
+        part[block] = jnp.dot(value, proj[...], preferred_element_type=f32).astype(bf16)
+
+    part_copies = []
+    for i in range(2):
+        block = (1 - core) + 2 * i
+        copy = pltpu.make_async_remote_copy(
+            src_ref=part.at[block],
+            dst_ref=part_in.at[i],
+            send_sem=part_send.at[i],
+            recv_sem=part_recv.at[i],
+            device_id={"tp": mate},
+            device_id_type=MESH,
+        )
+        copy.start()
+        part_copies.append(copy)
+    land_copies = []
+    for i in range(2):
+        block = core + 2 * i
+        part_copies[i].wait_recv()
+        halves[i] = (part[block].astype(f32) + part_in[i].astype(f32)).astype(bf16)
+        copy = pltpu.make_async_remote_copy(
+            src_ref=halves.at[i],
+            dst_ref=landed.at[side_x],
+            send_sem=land_send.at[i],
+            recv_sem=land_recv.at[side_x],
+            device_id={"ep": block, "tp": me},
+            device_id_type=MESH,
+        )
+        here = jnp.logical_and(block == me, me == lane)
+
+        @pl.when(here)
+        def _():
+            landed[side_x] = halves[i]
+
+        @pl.when(jnp.logical_not(here))
+        def _():
+            copy.start()
+
+        land_copies.append((copy, here))
+
+    for j in range(2):
+        source = 2 * j + lax.rem(me, 2)
+        mine = jnp.logical_and(me == lane, source == lane)
+
+        @pl.when(jnp.logical_not(mine))
+        def _():
+            pltpu.make_async_remote_copy(
+                src_ref=halves.at[0],
+                dst_ref=landed.at[j],
+                send_sem=land_send.at[0],
+                recv_sem=land_recv.at[j],
+                device_id={"tp": mate},
+                device_id_type=MESH,
+            ).wait_recv()
+
+    attention = landed[0].astype(f32) + landed[1].astype(f32)
+    hstate = (stream_ref[...].astype(f32) + attention).astype(bf16)
+    hkeep[...] = hstate
+    hfloat = hstate.astype(f32)
+    scaled = hfloat * gain_ref[...].astype(f32)
+    x_all[me] = scaled.astype(bf16)
+    x_copies = over_ep(x_all.at[me], x_all.at[me], x_send, x_recv)
+
+    side[...] = jnp.zeros_like(side)
+    side[:, 0:EXPERTS] = jnp.dot(
+        scaled, router_ref[...].astype(f32), precision=lax.Precision.HIGHEST, preferred_element_type=f32
+    )
+    side[:, EXPERTS : EXPERTS + 1] = jnp.sum(hfloat * hfloat, axis=1, keepdims=True)
+    side_copies = []
+    for k in range(1, n_tp):
+        copy = pltpu.make_async_remote_copy(
+            src_ref=side,
+            dst_ref=side_all.at[k - 1],
+            send_sem=side_send.at[k - 1],
+            recv_sem=side_recv.at[k - 1],
+            device_id={"tp": lax.rem(lane + k, n_tp)},
+            device_id_type=MESH,
+        )
+        copy.start()
+        side_copies.append(copy)
+    total = side[...]
+    for k in range(1, n_tp):
+        side_copies[k - 1].wait_recv()
+        total = total + side_all[k - 1]
+    inverse = lax.rsqrt(total[:, EXPERTS : EXPERTS + 1] / depth + 1e-05)
+    logits = total * inverse
+    first = jnp.sum(jnp.where(ids[:, 0:1] == lanes, logits, 0.0), axis=1, keepdims=True)
+    second = jnp.sum(jnp.where(ids[:, 1:2] == lanes, logits, 0.0), axis=1, keepdims=True)
+    leading = jax.nn.sigmoid(first - second)
+    inv_all[me] = jnp.broadcast_to(inverse, (tok, 128))
+    inv_copies = over_ep(inv_all.at[me], inv_all.at[me], inv_send, inv_recv)
+
+    for copy in slot_copies:
+        copy.wait_recv()
+    columns = []
+    wide = lax.broadcasted_iota(jnp.int32, (tok, 256), 1).astype(f32)
+    for b in range(n_ep):
+        picked = jnp.sum(jnp.where(lanes == me, slot_all[b], 0.0), axis=1, keepdims=True)
+        columns.append(jnp.where(picked + float(b * CAP) == wide, 1.0, 0.0).astype(f32))
+    chooser = jnp.transpose(jnp.concatenate(columns, axis=0))[:slots]
+    for copy in x_copies:
+        copy.wait_recv()
+    rows[...] = jnp.dot(
+        chooser.astype(bf16), x_all[...].reshape(n_ep * tok, width), preferred_element_type=f32
+    ).astype(bf16)
+    for copy in inv_copies:
+        copy.wait_recv()
+    inv_rows[...] = jnp.dot(
+        chooser,
+        inv_all[...].reshape(n_ep * tok, 128),
+        precision=lax.Precision.HIGHEST,
+        preferred_element_type=f32,
+    )
+    acc[...] = jnp.zeros_like(acc)
+    for name in ("g", "u", "d"):
+        for copy in loads[name]:
+            copy.wait()
+
+    def pair_copy(i):
+        return pltpu.make_async_remote_copy(
+            src_ref=pair_out.at[i], dst_ref=pair_in.at[i], send_sem=pair_send.at[i], recv_sem=pair_recv.at[i],
+            device_id={"tp": mate}, device_id_type=MESH,
+        )
+
+    def far_copy(i):
+        return pltpu.make_async_remote_copy(
+            src_ref=far_out.at[i], dst_ref=far_in.at[i], send_sem=far_send.at[i], recv_sem=far_recv.at[i],
+            device_id={"tp": across}, device_id_type=MESH,
+        )
+
+    own_q = 2 * core + side_x
+    far_q = 2 * core + (1 - side_x)
+
+    def hid_copy(i, q, target, sends, recvs):
+        return pltpu.make_async_remote_copy(
+            src_ref=hid.at[q, i], dst_ref=hid.at[q, i], send_sem=sends.at[i], recv_sem=recvs.at[i],
+            device_id={"tp": target}, device_id_type=MESH,
+        )
+
+    def columns_of(weight, q, i):
+        return weight[:, pl.ds(pl.multiple_of(q * quarter + i * CHUNK, CHUNK), CHUNK)]
+
+    def step(s, carry):
+        @pl.when(s < count)
+        def _():
+            i = s
+            value = rows[...]
+            for j in range(2):
+                for m, weight in enumerate((gate, up)):
+                    pair_out[i, 2 * j + m] = jnp.dot(
+                        value, columns_of(weight, 2 * (1 - core) + j, i), preferred_element_type=f32
+                    ).astype(bf16)
+            pair_copy(i).start()
+            for m, weight in enumerate((gate, up)):
+                own_far[lax.rem(i, 2), m] = jnp.dot(
+                    value, columns_of(weight, far_q, i), preferred_element_type=f32
+                )
+                own_near[i, m] = jnp.dot(
+                    value, columns_of(weight, own_q, i), preferred_element_type=f32
+                )
+
+        @pl.when(jnp.logical_and(s >= 1, s < count + 1))
+        def _():
+            i = s - 1
+            pair_copy(i).wait_recv()
+            for m in range(2):
+                far_out[i, m] = (
+                    own_far[lax.rem(i, 2), m] + pair_in[i, 2 * (1 - side_x) + m].astype(f32)
+                ).astype(bf16)
+            far_copy(i).start()
+            for m in range(2):
+                own_near[i, m] = own_near[i, m] + pair_in[i, 2 * side_x + m].astype(f32)
+
+        @pl.when(jnp.logical_and(s >= 3, s < count + 3))
+        def _():
+            i = s - 3
+            far_copy(i).wait_recv()
+            scale = inv_rows[:, 0:1]
+            g = (own_near[i, 0] + far_in[i, 0].astype(f32)) * scale
+            u = (own_near[i, 1] + far_in[i, 1].astype(f32)) * scale
+            hid[own_q, i] = (g / (1.0 + jnp.exp(-g)) * u).astype(bf16)
+            hid_copy(i, own_q, across, hx_send, hx_recv).start()
+            hid_copy(i, own_q, mate, hc_send, hc_recv).start()
+
+        @pl.when(jnp.logical_and(s >= 4, s < count + 4))
+        def _():
+            i = s - 4
+            hid_copy(i, far_q, across, hx_send, hx_recv).wait_recv()
+            hid_copy(i, far_q, mate, hf_send, hf_recv).start()
+
+        @pl.when(s >= 5)
+        def _():
+            i = s - 5
+            hid_copy(i, own_q, mate, hc_send, hc_recv).wait_recv()
+            hid_copy(i, far_q, mate, hf_send, hf_recv).wait_recv()
+            value = acc[...]
+            for q in range(4):
+                value = value + jnp.dot(
+                    hid[q, i],
+                    down[pl.ds(pl.multiple_of(q * quarter + i * CHUNK, CHUNK), CHUNK), :],
+                    preferred_element_type=f32,
+                )
+            acc[...] = value
+
+        return carry
+
+    lax.fori_loop(0, count + 5, step, 0)
+
+    outb[...] = acc[...].astype(bf16)
+    ret_copies = []
+    for k in range(1, n_ep):
+        peer = lax.rem(me + k, n_ep)
+        copy = pltpu.make_async_remote_copy(
+            src_ref=outb.at[pl.ds(pl.multiple_of(peer * (CAP // 16 * 16), 16), WINDOW)],
+            dst_ref=ret.at[me],
+            send_sem=ret_send.at[k - 1],
+            recv_sem=ret_recv.at[k - 1],
+            device_id={"ep": peer},
+            device_id_type=MESH,
+        )
+        copy.start()
+        ret_copies.append(copy)
+    ret[me] = outb[pl.ds(pl.multiple_of(me * (CAP // 16 * 16), 16), WINDOW), :]
+    shift = (me * (CAP - CAP // 16 * 16)).astype(f32)
+    window = lax.broadcasted_iota(jnp.int32, (tok, WINDOW), 1).astype(f32)
+
+    def returned(source):
+        at_source = lanes == source
+        place = jnp.sum(jnp.where(at_source, slot_all[me], 0.0), axis=1, keepdims=True) + shift
+        chosen = jnp.where(place == window, 1.0, 0.0).astype(bf16)
+        weight = jnp.where(
+            ids[:, 0:1] == source, leading, jnp.where(ids[:, 1:2] == source, 1.0 - leading, 0.0)
+        )
+        return weight * jnp.dot(chosen, ret[source], preferred_element_type=f32)
+
+    mixed = hkeep[...].astype(f32) + returned(me)
+    for k in range(1, n_ep):
+        ret_copies[k - 1].wait_recv()
+        mixed = mixed + returned(lax.rem(me + n_ep - k, n_ep))
+    out_ref[...] = mixed.astype(bf16)
+
+    for copy in ctx_copies + slot_copies + part_copies + side_copies + x_copies + inv_copies + ret_copies:
+        copy.wait_send()
+    for copy, here in land_copies:
+
+        @pl.when(jnp.logical_not(here))
+        def _():
+            copy.wait_send()
+
+    def drain(i, carry):
+        pair_copy(i).wait_send()
+        far_copy(i).wait_send()
+        hid_copy(i, own_q, across, hx_send, hx_recv).wait_send()
+        hid_copy(i, own_q, mate, hc_send, hc_recv).wait_send()
+        hid_copy(i, far_q, mate, hf_send, hf_recv).wait_send()
+        return carry
+
+    lax.fori_loop(0, count, drain, 0)
+
+
+def fused_device(context, stream, out_proj, norm_gain, router, expert_ids, w_gate, w_up, w_down):
+    n_ep, n_tp = lax.axis_size("ep"), lax.axis_size("tp")
+    tok, width = stream.shape
+    heads = context.shape[1]
+    hidden = w_gate.shape[1]
+    cols = out_proj.shape[1]
+    slots = n_ep * CAP
+    count = hidden // n_tp // CHUNK
+    pieces = 4
+    bf16, f32 = jnp.bfloat16, jnp.float32
+    vmem, hbm = pl.BlockSpec(memory_space=pltpu.VMEM), pl.BlockSpec(memory_space=pl.ANY)
+    dma = lambda n: pltpu.SemaphoreType.DMA((n,))
+    scratch = [
+        pltpu.VMEM(out_proj.shape, bf16),
+        pltpu.VMEM(w_gate.shape, bf16),
+        pltpu.VMEM(w_up.shape, bf16),
+        pltpu.VMEM(w_down.shape, bf16),
+        pltpu.VMEM((n_ep, tok, heads), bf16),
+        pltpu.VMEM((n_ep, tok, cols), bf16),
+        pltpu.VMEM((2, tok, cols), bf16),
+        pltpu.VMEM((2, tok, cols), bf16),
+        pltpu.VMEM((2, tok, cols), bf16),
+        pltpu.VMEM((tok, width), bf16),
+        pltpu.VMEM((n_ep, tok, width), bf16),
+        pltpu.VMEM((slots, width), bf16),
+        pltpu.VMEM((tok, 128), f32),
+        pltpu.VMEM((n_tp - 1, tok, 128), f32),
+        pltpu.VMEM((n_ep, tok, 128), f32),
+        pltpu.VMEM((n_ep, tok, 128), f32),
+        pltpu.VMEM((slots, 128), f32),
+        pltpu.VMEM((count, 4, slots, CHUNK), bf16),
+        pltpu.VMEM((count, 4, slots, CHUNK), bf16),
+        pltpu.VMEM((2, 2, slots, CHUNK), f32),
+        pltpu.VMEM((count, 2, slots, CHUNK), f32),
+        pltpu.VMEM((count, 2, slots, CHUNK), bf16),
+        pltpu.VMEM((count, 2, slots, CHUNK), bf16),
+        pltpu.VMEM((4, count, slots, CHUNK), bf16),
+        pltpu.VMEM((slots, width), f32),
+        pltpu.VMEM((slots, width), bf16),
+        pltpu.VMEM((n_ep, WINDOW, width), bf16),
+        dma(4 * pieces),
+    ]
+    for size in (n_ep - 1, n_ep - 1, 2, 2, n_tp - 1, n_ep - 1, n_ep - 1, count, count, count, count, count, n_ep - 1):
+        scratch += [dma(size), dma(size)]
+    return pl.pallas_call(
+        functools.partial(fused_kernel, n_ep, n_tp, pieces),
+        out_shape=jax.ShapeDtypeStruct((tok, width), bf16),
+        in_specs=[vmem] * 5 + [hbm] * 4,
+        out_specs=vmem,
+        scratch_shapes=scratch,
+        compiler_params=pltpu.CompilerParams(
+            collective_id=0, has_side_effects=True, vmem_limit_bytes=VMEM_BYTES
+        ),
+        name="fused_layer",
+    )(context, stream, norm_gain.reshape(1, width), router, expert_ids, out_proj, w_gate, w_up, w_down)
+
+
 def solution(mesh):
+    sizes = dict(mesh.shape)
+    fused = sizes["tp"] == 4 and sizes["ep"] == EXPERTS
     return jax.shard_map(
-        per_device,
+        fused_device if fused else plain_device,
         mesh=mesh,
         in_specs=(
             P(("groups", "ep"), "tp"),

time: 224 us -> 101 us (0.45)
  waiting for transfers between devices: 103 us -> 0 us
  Pallas kernels: 0 us -> 94.7 us
  blocking collectives: 74.5 us -> 0 us
  matrix products: 29.1 us -> 0 us
  between operations: 13.5 us -> 0.01 us
  local copies, waits for them, and re-layouts: 1.54 us -> 5.78 us
    pallas_call x0 -> x1, Pallas kernels: none -> 94.7 us  [fused_device(): pl.pallas_call(functools.partial(fused_kernel, n_ep, n_tp, pieces), out_s...]
    psum x1 -> x0, waiting for transfers between devices: 83.2 us -> none  [per_device(): up_sum = lax.psum(up_part.astype(jnp.bfloat16), 'tp').astype(jnp.float32)]
    all_to_all x3 -> x0, blocking collectives: 45.3 us -> none  [the longest x1 16.1 us: per_device(): lax.all_to_all(columns.astype(jnp.bfloat16), 'ep', split_axis=0, concat_a...]
    dot_general x7 -> x0, matrix products: 29.1 us -> none  [the longest x1 9.22 us: per_device(): jnp.dot(hidden, w_down, preferred_element_type=jnp.float32)]
    reduce_scatter x1 -> x0, waiting for transfers between devices: 19.9 us -> none  [per_device(): lax.psum_scatter(head_part, 'tp', scatter_dimension=1, tiled=True)]
    all_gather x1 -> x0, blocking collectives: 17.7 us -> none  [per_device(): lax.all_gather(context, 'ep', axis=0, tiled=True)]
    psum x2 -> x0, blocking collectives: 11.4 us -> none  [the longest x1 5.76 us: per_device(): total_sq = lax.psum(squares, 'tp')]
    unnamed x11 -> x3, local copies, waits for them, and re-layouts: 0.12 us -> 4.52 us
  transfers between devices with their start and end apart: 2 -> 0, of which waited for: 2 -> 0; matrix products, arithmetic and copies ran while one was open for 0% -> 0% of each run, Pallas kernels for 0% -> 0%
where the time goes in v1:
time: 101 us; the launch traced here: 100 us
  Pallas kernels  94.7 us (94%)
  local copies, waits for them, and re-layouts  5.78 us (6%)
    pallas_call x1, Pallas kernels, fused_device(): pl.pallas_call(functools.partial(fused_kernel, n_ep, n_tp, pieces), out_s...  94.7 us
    unnamed x3, local copies, waits for them, and re-layouts  4.52 us

profile of v1, /device:TPU:0, one launch (start us, length us, event | category | flops | bytes accessed | tf_op | source)
XLA Modules:
  0.0 100.5 jit_solution(14121773031608126005)
XLA Ops:
  0.0 1.3 %reshape.3.gain_ref = bf16[1,1024]{1,0:T(2,128)(2,1)} reshape(bf16[1024]{0:T(1024)(128)(2,1)} %param.12) | data formatting | bytes 4096 | tf_op jit(solution)/shard_map/reshape | solution.py:557
  1.3 1.4 %copy.11.ids_ref = s32[64,2]{1,0:T(8,128)} copy(s32[64,2]{0,1:T(2,128)} %param.14) | data formatting | bytes 1024 | tf_op args[5]
  2.7 1.6 %copy.10.router_ref = bf16[1024,4]{1,0:T(8,128)(2,1)} copy(bf16[1024,4]{0,1:T(4,128)(2,1)} %param.13) | data formatting | bytes 16384 | tf_op args[4]
  4.2 94.7 %fused_layer.1 = bf16[64,1024]{1,0:T(8,128)(2,1)} custom-call(bf16[64,1024]{1,0:T(8,128)(2,1)} %ctx_ref.1, bf16[64,1024]{1,0:T(8,128)(2,1)} %stream_ref.1, bf16[1,1024]{1,0:T(2,128)(2,1)} %reshape.3.gain_ref, bf16[1024,4]{1,0:T(8,128)(2,1)} %copy.10.router_ref, s32[64,2]{1,0:T(8,128)} %copy.11.ids_ref, bf16[1024,1024]{1,0:T(8,128)(2,1)} %proj_hbm.1, ...), custom_call_target="tpu_custom_call" | custom-call | tf_op jit(solution)/shard_map/fused_layer/pallas_call | solution.py:547
  98.9 1.6 %copy.13 = bf16[64,1024]{1,0:T(8,128)(2,1)} copy(bf16[64,1024]{1,0:T(8,128)(2,1)} %fused_layer.1) | data formatting | bytes 262144

commit v2 on v1

--- a/solution.py
+++ b/solution.py
@@ -90,7 +90,9 @@
 
 MESH = pl.DeviceIdType.MESH
 CHUNK = 256
-WINDOW = 48
+LAG_SUM, LAG_PASS, LAG_DOWN = 4, 7, 9
+WINDOW = 40
+ALIGN = 8
 VMEM_BYTES = 67043328
 
 
@@ -125,6 +127,8 @@
     inv_all,
     slot_all,
     inv_rows,
+    chooser,
+    mix,
     pair_out,
     pair_in,
     own_far,
@@ -173,8 +177,10 @@
     depth = n_tp * width
     quarter = gate.shape[1] // n_tp
     count = quarter // CHUNK
-    slots = rows.shape[0]
+    total_steps = 2 * count
+    slots = rows.shape[1]
     f32, bf16 = jnp.float32, jnp.bfloat16
+    peers = (me, me + 1 - 2 * lax.rem(me, 2), lax.rem(me + 2, 4), 3 - me)
 
     loads = {}
     number = 0
@@ -201,15 +207,16 @@
                     device_id_type=MESH,
                 )
 
-    ids = ids_ref[...]
+    experts = lax.broadcasted_iota(jnp.int32, (128, tok), 0)
+    is_first = jnp.transpose(jnp.where(ids_ref[0:1, :] == experts, 1.0, 0.0).astype(f32))
+    is_second = jnp.transpose(jnp.where(ids_ref[1:2, :] == experts, 1.0, 0.0).astype(f32))
+    named = is_first + is_second
     lanes = lax.broadcasted_iota(jnp.int32, (tok, 128), 1)
-    named = jnp.where((ids[:, 0:1] == lanes) | (ids[:, 1:2] == lanes), 1.0, 0.0).astype(f32)
     row_i = lax.broadcasted_iota(jnp.int32, (tok, tok), 0)
     col_i = lax.broadcasted_iota(jnp.int32, (tok, tok), 1)
     lower = jnp.where(col_i < row_i, 1.0, 0.0).astype(bf16)
     rank = jnp.dot(lower, named.astype(bf16), preferred_element_type=f32)
-    slot_local = jnp.where(named > 0.5, rank, -4096.0)
-    slot_all[me] = slot_local
+    slot_all[0] = jnp.where(named > 0.5, rank, -4096.0)
 
     pl.semaphore_wait(barrier, n_ep * n_tp - 1)
 
@@ -218,35 +225,33 @@
         for k in range(1, n_ep):
             copy = pltpu.make_async_remote_copy(
                 src_ref=src,
-                dst_ref=dst,
+                dst_ref=dst.at[k],
                 send_sem=sends.at[k - 1],
                 recv_sem=recvs.at[k - 1],
-                device_id={"ep": lax.rem(me + k, n_ep)},
+                device_id={"ep": peers[k]},
                 device_id_type=MESH,
             )
             copy.start()
             copies.append(copy)
         return copies
 
-    ctx_copies = over_ep(ctx_ref, ctx_all.at[me], ctx_send, ctx_recv)
-    slot_copies = over_ep(slot_all.at[me], slot_all.at[me], slot_send, slot_recv)
+    ctx_copies = over_ep(ctx_ref, ctx_all, ctx_send, ctx_recv)
+    slot_copies = over_ep(slot_all.at[0], slot_all, slot_send, slot_recv)
 
     for copy in loads["p"]:
         copy.wait()
-    for k in range(n_ep):
-        block = lax.rem(me + n_ep - k, n_ep)
-        if k:
-            ctx_copies[k - 1].wait_recv()
-            value = ctx_all[block]
-        else:
-            value = ctx_ref[...]
-        part[block] = jnp.dot(value, proj[...], preferred_element_type=f32).astype(bf16)
-
-    part_copies = []
+    part_copies, land_copies = [], []
     for i in range(2):
-        block = (1 - core) + 2 * i
+        pair = me // 2 if i == 0 else 1 - me // 2
+        for k in (2 * i, 2 * i + 1):
+            if k:
+                ctx_copies[k - 1].wait_recv()
+                value = ctx_all[k]
+            else:
+                value = ctx_ref[...]
+            part[peers[k]] = jnp.dot(value, proj[...], preferred_element_type=f32).astype(bf16)
         copy = pltpu.make_async_remote_copy(
-            src_ref=part.at[block],
+            src_ref=part.at[2 * pair + (1 - core)],
             dst_ref=part_in.at[i],
             send_sem=part_send.at[i],
             recv_sem=part_recv.at[i],
@@ -255,10 +260,8 @@
         )
         copy.start()
         part_copies.append(copy)
-    land_copies = []
-    for i in range(2):
-        block = core + 2 * i
-        part_copies[i].wait_recv()
+        block = 2 * pair + core
+        copy.wait_recv()
         halves[i] = (part[block].astype(f32) + part_in[i].astype(f32)).astype(bf16)
         copy = pltpu.make_async_remote_copy(
             src_ref=halves.at[i],
@@ -299,13 +302,17 @@
     hstate = (stream_ref[...].astype(f32) + attention).astype(bf16)
     hkeep[...] = hstate
     hfloat = hstate.astype(f32)
-    scaled = hfloat * gain_ref[...].astype(f32)
-    x_all[me] = scaled.astype(bf16)
-    x_copies = over_ep(x_all.at[me], x_all.at[me], x_send, x_recv)
+    scaled = hfloat * gain_ref[...].astype(f32).reshape(1, width)
+    x_all[0] = scaled.astype(bf16)
+    x_copies = over_ep(x_all.at[0], x_all, x_send, x_recv)
 
     side[...] = jnp.zeros_like(side)
-    side[:, 0:EXPERTS] = jnp.dot(
-        scaled, router_ref[...].astype(f32), precision=lax.Precision.HIGHEST, preferred_element_type=f32
+    side[:, 0:EXPERTS] = lax.dot_general(
+        scaled,
+        router_ref[...].astype(f32),
+        (((1,), (1,)), ((), ())),
+        precision=lax.Precision.HIGHEST,
+        preferred_element_type=f32,
     )
     side[:, EXPERTS : EXPERTS + 1] = jnp.sum(hfloat * hfloat, axis=1, keepdims=True)
     side_copies = []
@@ -326,37 +333,54 @@
         total = total + side_all[k - 1]
     inverse = lax.rsqrt(total[:, EXPERTS : EXPERTS + 1] / depth + 1e-05)
     logits = total * inverse
-    first = jnp.sum(jnp.where(ids[:, 0:1] == lanes, logits, 0.0), axis=1, keepdims=True)
-    second = jnp.sum(jnp.where(ids[:, 1:2] == lanes, logits, 0.0), axis=1, keepdims=True)
+    first = jnp.sum(is_first * logits, axis=1, keepdims=True)
+    second = jnp.sum(is_second * logits, axis=1, keepdims=True)
     leading = jax.nn.sigmoid(first - second)
-    inv_all[me] = jnp.broadcast_to(inverse, (tok, 128))
-    inv_copies = over_ep(inv_all.at[me], inv_all.at[me], inv_send, inv_recv)
+    mix[...] = is_first * leading + is_second * (1.0 - leading)
+    inv_all[0] = jnp.broadcast_to(inverse, (tok, 128))
+    inv_copies = over_ep(inv_all.at[0], inv_all, inv_send, inv_recv)
 
     for copy in slot_copies:
         copy.wait_recv()
-    columns = []
-    wide = lax.broadcasted_iota(jnp.int32, (tok, 256), 1).astype(f32)
-    for b in range(n_ep):
-        picked = jnp.sum(jnp.where(lanes == me, slot_all[b], 0.0), axis=1, keepdims=True)
-        columns.append(jnp.where(picked + float(b * CAP) == wide, 1.0, 0.0).astype(f32))
-    chooser = jnp.transpose(jnp.concatenate(columns, axis=0))[:slots]
-    for copy in x_copies:
-        copy.wait_recv()
-    rows[...] = jnp.dot(
-        chooser.astype(bf16), x_all[...].reshape(n_ep * tok, width), preferred_element_type=f32
-    ).astype(bf16)
-    for copy in inv_copies:
-        copy.wait_recv()
-    inv_rows[...] = jnp.dot(
-        chooser,
-        inv_all[...].reshape(n_ep * tok, 128),
-        precision=lax.Precision.HIGHEST,
-        preferred_element_type=f32,
-    )
+    wide = lanes.astype(f32)
+    for g in range(2):
+        columns = []
+        for p in range(2):
+            picked = jnp.sum(jnp.where(lanes == me, slot_all[2 * g + p], 0.0), axis=1, keepdims=True)
+            columns.append(jnp.where(picked + float(p * CAP) == wide, 1.0, 0.0).astype(f32))
+        chooser[g] = jnp.transpose(jnp.concatenate(columns, axis=0))[:slots]
+
+    def fill_rows(g):
+        rows[g] = jnp.dot(
+            chooser[g].astype(bf16),
+            x_all[2 * g : 2 * g + 2].reshape(2 * tok, width),
+            preferred_element_type=f32,
+        ).astype(bf16)
+
+    def fill_inverse(g):
+        inv_rows[g] = jnp.dot(
+            chooser[g],
+            inv_all[2 * g : 2 * g + 2].reshape(2 * tok, 128),
+            precision=lax.Precision.HIGHEST,
+            preferred_element_type=f32,
+        )
+
     acc[...] = jnp.zeros_like(acc)
     for name in ("g", "u", "d"):
         for copy in loads[name]:
             copy.wait()
+    x_copies[0].wait_recv()
+    fill_rows(0)
+
+    def ret_copy(k):
+        return pltpu.make_async_remote_copy(
+            src_ref=outb.at[k // 2, pl.ds((k % 2) * (CAP // ALIGN * ALIGN), WINDOW)],
+            dst_ref=ret.at[k],
+            send_sem=ret_send.at[k - 1],
+            recv_sem=ret_recv.at[k - 1],
+            device_id={"ep": peers[k]},
+            device_id_type=MESH,
+        )
 
     def pair_copy(i):
         return pltpu.make_async_remote_copy(
@@ -380,13 +404,19 @@
         )
 
     def columns_of(weight, q, i):
-        return weight[:, pl.ds(pl.multiple_of(q * quarter + i * CHUNK, CHUNK), CHUNK)]
+        return weight[:, pl.ds(pl.multiple_of(q * quarter + lax.rem(i, count) * CHUNK, CHUNK), CHUNK)]
 
     def step(s, carry):
-        @pl.when(s < count)
+        @pl.when(s == count)
+        def _():
+            for k in (2, 3):
+                x_copies[k - 1].wait_recv()
+            fill_rows(1)
+
+        @pl.when(s < total_steps)
         def _():
             i = s
-            value = rows[...]
+            value = rows[i // count]
             for j in range(2):
                 for m, weight in enumerate((gate, up)):
                     pair_out[i, 2 * j + m] = jnp.dot(
@@ -401,7 +431,7 @@
                     value, columns_of(weight, own_q, i), preferred_element_type=f32
                 )
 
-        @pl.when(jnp.logical_and(s >= 1, s < count + 1))
+        @pl.when(jnp.logical_and(s >= 1, s < total_steps + 1))
         def _():
             i = s - 1
             pair_copy(i).wait_recv()
@@ -413,75 +443,81 @@
             for m in range(2):
                 own_near[i, m] = own_near[i, m] + pair_in[i, 2 * side_x + m].astype(f32)
 
-        @pl.when(jnp.logical_and(s >= 3, s < count + 3))
-        def _():
-            i = s - 3
+        @pl.when(s == LAG_SUM)
+        def _():
+            inv_copies[0].wait_recv()
+            fill_inverse(0)
+
+        @pl.when(s == count + LAG_SUM)
+        def _():
+            for k in (2, 3):
+                inv_copies[k - 1].wait_recv()
+            fill_inverse(1)
+
+        @pl.when(jnp.logical_and(s >= LAG_SUM, s < total_steps + LAG_SUM))
+        def _():
+            i = s - LAG_SUM
             far_copy(i).wait_recv()
-            scale = inv_rows[:, 0:1]
+            scale = inv_rows[i // count, :, 0:1]
             g = (own_near[i, 0] + far_in[i, 0].astype(f32)) * scale
             u = (own_near[i, 1] + far_in[i, 1].astype(f32)) * scale
             hid[own_q, i] = (g / (1.0 + jnp.exp(-g)) * u).astype(bf16)
             hid_copy(i, own_q, across, hx_send, hx_recv).start()
             hid_copy(i, own_q, mate, hc_send, hc_recv).start()
 
-        @pl.when(jnp.logical_and(s >= 4, s < count + 4))
-        def _():
-            i = s - 4
+        @pl.when(jnp.logical_and(s >= LAG_PASS, s < total_steps + LAG_PASS))
+        def _():
+            i = s - LAG_PASS
             hid_copy(i, far_q, across, hx_send, hx_recv).wait_recv()
             hid_copy(i, far_q, mate, hf_send, hf_recv).start()
 
-        @pl.when(s >= 5)
-        def _():
-            i = s - 5
+        @pl.when(s >= LAG_DOWN)
+        def _():
+            i = s - LAG_DOWN
             hid_copy(i, own_q, mate, hc_send, hc_recv).wait_recv()
             hid_copy(i, far_q, mate, hf_send, hf_recv).wait_recv()
             value = acc[...]
             for q in range(4):
                 value = value + jnp.dot(
                     hid[q, i],
-                    down[pl.ds(pl.multiple_of(q * quarter + i * CHUNK, CHUNK), CHUNK), :],
+                    down[pl.ds(pl.multiple_of(q * quarter + lax.rem(i, count) * CHUNK, CHUNK), CHUNK), :],
                     preferred_element_type=f32,
                 )
             acc[...] = value
 
+            @pl.when(i == count - 1)
+            def _():
+                outb[0] = acc[...].astype(bf16)
+                ret_copy(1).start()
+                acc[...] = jnp.zeros_like(acc)
+
         return carry
 
-    lax.fori_loop(0, count + 5, step, 0)
-
-    outb[...] = acc[...].astype(bf16)
-    ret_copies = []
+    lax.fori_loop(0, total_steps + LAG_DOWN, step, 0)
+
+    outb[1] = acc[...].astype(bf16)
+    for k in (2, 3):
+        ret_copy(k).start()
+    window = lax.broadcasted_iota(jnp.int32, (tok, WINDOW), 1).astype(f32)
+
+    def returned(k):
+        at_source = lanes == peers[k]
+        shift = float((k % 2) * (CAP - CAP // ALIGN * ALIGN))
+        place = jnp.sum(jnp.where(at_source, slot_all[0], 0.0), axis=1, keepdims=True) + shift
+        chosen = jnp.where(place == window, 1.0, 0.0).astype(bf16)
+        weight = jnp.sum(jnp.where(at_source, mix[...], 0.0), axis=1, keepdims=True)
+        value = outb[0, 0:WINDOW, :] if k == 0 else ret[k]
+        return weight * jnp.dot(chosen, value, preferred_element_type=f32)
+
+    mixed = hkeep[...].astype(f32) + returned(0)
     for k in range(1, n_ep):
-        peer = lax.rem(me + k, n_ep)
-        copy = pltpu.make_async_remote_copy(
-            src_ref=outb.at[pl.ds(pl.multiple_of(peer * (CAP // 16 * 16), 16), WINDOW)],
-            dst_ref=ret.at[me],
-            send_sem=ret_send.at[k - 1],
-            recv_sem=ret_recv.at[k - 1],
-            device_id={"ep": peer},
-            device_id_type=MESH,
-        )
-        copy.start()
-        ret_copies.append(copy)
-    ret[me] = outb[pl.ds(pl.multiple_of(me * (CAP // 16 * 16), 16), WINDOW), :]
-    shift = (me * (CAP - CAP // 16 * 16)).astype(f32)
-    window = lax.broadcasted_iota(jnp.int32, (tok, WINDOW), 1).astype(f32)
-
-    def returned(source):
-        at_source = lanes == source
-        place = jnp.sum(jnp.where(at_source, slot_all[me], 0.0), axis=1, keepdims=True) + shift
-        chosen = jnp.where(place == window, 1.0, 0.0).astype(bf16)
-        weight = jnp.where(
-            ids[:, 0:1] == source, leading, jnp.where(ids[:, 1:2] == source, 1.0 - leading, 0.0)
-        )
-        return weight * jnp.dot(chosen, ret[source], preferred_element_type=f32)
-
-    mixed = hkeep[...].astype(f32) + returned(me)
+        ret_copy(k).wait_recv()
+        mixed = mixed + returned(k)
+    out_ref[...] = mixed.astype(bf16)
     for k in range(1, n_ep):
-        ret_copies[k - 1].wait_recv()
-        mixed = mixed + returned(lax.rem(me + n_ep - k, n_ep))
-    out_ref[...] = mixed.astype(bf16)
-
-    for copy in ctx_copies + slot_copies + part_copies + side_copies + x_copies + inv_copies + ret_copies:
+        ret_copy(k).wait_send()
+
+    for copy in ctx_copies + slot_copies + part_copies + side_copies + x_copies + inv_copies:
         copy.wait_send()
     for copy, here in land_copies:
 
@@ -497,7 +533,7 @@
         hid_copy(i, far_q, mate, hf_send, hf_recv).wait_send()
         return carry
 
-    lax.fori_loop(0, count, drain, 0)
+    lax.fori_loop(0, total_steps, drain, 0)
 
 
 def fused_device(context, stream, out_proj, norm_gain, router, expert_ids, w_gate, w_up, w_down):
@@ -506,8 +542,8 @@
     heads = context.shape[1]
     hidden = w_gate.shape[1]
     cols = out_proj.shape[1]
-    slots = n_ep * CAP
-    count = hidden // n_tp // CHUNK
+    slots = 2 * CAP
+    count = 2 * (hidden // n_tp // CHUNK)
     pieces = 4
     bf16, f32 = jnp.bfloat16, jnp.float32
     vmem, hbm = pl.BlockSpec(memory_space=pltpu.VMEM), pl.BlockSpec(memory_space=pl.ANY)
@@ -524,12 +560,14 @@
         pltpu.VMEM((2, tok, cols), bf16),
         pltpu.VMEM((tok, width), bf16),
         pltpu.VMEM((n_ep, tok, width), bf16),
-        pltpu.VMEM((slots, width), bf16),
+        pltpu.VMEM((2, slots, width), bf16),
         pltpu.VMEM((tok, 128), f32),
         pltpu.VMEM((n_tp - 1, tok, 128), f32),
         pltpu.VMEM((n_ep, tok, 128), f32),
         pltpu.VMEM((n_ep, tok, 128), f32),
-        pltpu.VMEM((slots, 128), f32),
+        pltpu.VMEM((2, slots, 128), f32),
+        pltpu.VMEM((2, slots, 2 * tok), f32),
+        pltpu.VMEM((tok, 128), f32),
         pltpu.VMEM((count, 4, slots, CHUNK), bf16),
         pltpu.VMEM((count, 4, slots, CHUNK), bf16),
         pltpu.VMEM((2, 2, slots, CHUNK), f32),
@@ -538,7 +576,7 @@
         pltpu.VMEM((count, 2, slots, CHUNK), bf16),
         pltpu.VMEM((4, count, slots, CHUNK), bf16),
         pltpu.VMEM((slots, width), f32),
-        pltpu.VMEM((slots, width), bf16),
+        pltpu.VMEM((2, slots, width), bf16),
         pltpu.VMEM((n_ep, WINDOW, width), bf16),
         dma(4 * pieces),
     ]
@@ -554,7 +592,7 @@
             collective_id=0, has_side_effects=True, vmem_limit_bytes=VMEM_BYTES
         ),
         name="fused_layer",
-    )(context, stream, norm_gain.reshape(1, width), router, expert_ids, out_proj, w_gate, w_up, w_down)
+    )(context, stream, norm_gain, router.T, expert_ids.T, out_proj, w_gate, w_up, w_down)
 
 
 def solution(mesh):

time: 101 us -> 89.4 us (0.89)
  Pallas kernels: 94.7 us -> 87.6 us
  local copies, waits for them, and re-layouts: 5.78 us -> 1.57 us
    pallas_call x1, Pallas kernels: 94.7 us -> 87.6 us  [fused_device(): pl.pallas_call(functools.partial(fused_kernel, n_ep, n_tp, pieces), out_s...]
    unnamed x3 -> x1, local copies, waits for them, and re-layouts: 4.52 us -> 1.57 us
    reshape x1 -> x0, local copies, waits for them, and re-layouts: 1.27 us -> none  [fused_device(): norm_gain.reshape(1, width)]
where the time goes in v2:
time: 89.4 us; the launch traced here: 89.2 us
  Pallas kernels  87.6 us (98%)
  local copies, waits for them, and re-layouts  1.57 us (2%)
    pallas_call x1, Pallas kernels, fused_device(): pl.pallas_call(functools.partial(fused_kernel, n_ep, n_tp, pieces), out_s...  87.6 us

profile of v2, /device:TPU:0, one launch (start us, length us, event | category | flops | bytes accessed | tf_op | source)
XLA Modules:
  0.0 89.2 jit_solution(6849066330750395271)
XLA Ops:
  0.0 87.6 %fused_layer.1 = bf16[64,1024]{1,0:T(8,128)(2,1)} custom-call(bf16[64,1024]{1,0:T(8,128)(2,1)} %ctx_ref.1, bf16[64,1024]{1,0:T(8,128)(2,1)} %stream_ref.1, bf16[1024]{0:T(1024)(128)(2,1)} %gain_ref.1, bf16[4,1024]{1,0:T(4,128)(2,1)} %bitcast.2, s32[2,64]{1,0:T(2,128)} %bitcast.3, bf16[1024,1024]{1,0:T(8,128)(2,1)} %proj_hbm.1, bf16[1024,7168]{1,0:T(8,128)(2,1)} %gate_hbm.1, ...), custom_call_target="tpu_custom_call" | custom-call | tf_op jit(solution)/shard_map/fused_layer/pallas_call | solution.py:585
  87.6 1.6 %copy.11 = bf16[64,1024]{1,0:T(8,128)(2,1)} copy(bf16[64,1024]{1,0:T(8,128)(2,1)} %fused_layer.1) | data formatting | bytes 262144

commit v3 on v2

--- a/solution.py
+++ b/solution.py
@@ -283,6 +283,16 @@
 
         land_copies.append((copy, here))
 
+    for copy in slot_copies:
+        copy.wait_recv()
+    wide = lanes.astype(f32)
+    for g in range(2):
+        columns = []
+        for p in range(2):
+            picked = jnp.sum(jnp.where(lanes == me, slot_all[2 * g + p], 0.0), axis=1, keepdims=True)
+            columns.append(jnp.where(picked + float(p * CAP) == wide, 1.0, 0.0).astype(f32))
+        chooser[g] = jnp.transpose(jnp.concatenate(columns, axis=0))[:slots]
+
     for j in range(2):
         source = 2 * j + lax.rem(me, 2)
         mine = jnp.logical_and(me == lane, source == lane)
@@ -339,16 +349,6 @@
     mix[...] = is_first * leading + is_second * (1.0 - leading)
     inv_all[0] = jnp.broadcast_to(inverse, (tok, 128))
     inv_copies = over_ep(inv_all.at[0], inv_all, inv_send, inv_recv)
-
-    for copy in slot_copies:
-        copy.wait_recv()
-    wide = lanes.astype(f32)
-    for g in range(2):
-        columns = []
-        for p in range(2):
-            picked = jnp.sum(jnp.where(lanes == me, slot_all[2 * g + p], 0.0), axis=1, keepdims=True)
-            columns.append(jnp.where(picked + float(p * CAP) == wide, 1.0, 0.0).astype(f32))
-        chooser[g] = jnp.transpose(jnp.concatenate(columns, axis=0))[:slots]
 
     def fill_rows(g):
         rows[g] = jnp.dot(

time: 89.4 us -> 89.9 us (level)
  no operation moved by 1% of the time
where the time goes in v3:
time: 89.9 us; the launch traced here: 89.7 us
  Pallas kernels  88.1 us (98%)
  local copies, waits for them, and re-layouts  1.57 us (2%)
    pallas_call x1, Pallas kernels, fused_device(): pl.pallas_call(functools.partial(fused_kernel, n_ep, n_tp, pieces), out_s...  88.1 us

profile of v3, /device:TPU:0, one launch (start us, length us, event | category | flops | bytes accessed | tf_op | source)
XLA Modules:
  0.0 89.7 jit_solution(12943011021145762048)
XLA Ops:
  0.0 88.1 %fused_layer.1 = bf16[64,1024]{1,0:T(8,128)(2,1)} custom-call(bf16[64,1024]{1,0:T(8,128)(2,1)} %ctx_ref.1, bf16[64,1024]{1,0:T(8,128)(2,1)} %stream_ref.1, bf16[1024]{0:T(1024)(128)(2,1)} %gain_ref.1, bf16[4,1024]{1,0:T(4,128)(2,1)} %bitcast.2, s32[2,64]{1,0:T(2,128)} %bitcast.3, bf16[1024,1024]{1,0:T(8,128)(2,1)} %proj_hbm.1, bf16[1024,7168]{1,0:T(8,128)(2,1)} %gate_hbm.1, ...), custom_call_target="tpu_custom_call" | custom-call | tf_op jit(solution)/shard_map/fused_layer/pallas_call | solution.py:585
  88.1 1.6 %copy.11 = bf16[64,1024]{1,0:T(8,128)(2,1)} copy(bf16[64,1024]{1,0:T(8,128)(2,1)} %fused_layer.1) | data formatting | bytes 262144
